TPU v7x, 512 devices: a whole 4x8x8 slice. The times are simulated.
512 devices in a mesh: dp: 32 (over y_lo, z), owner: 16 (over x, y_hi, core).
Axes of the slice: x: 4, y: 8 (y_hi: 2, y_lo: 4; y = y_hi * 4 + y_lo), z: 8, core: 2. Of those that a mesh axis runs over, the one named last changes fastest.
Arguments:
- gradients: bfloat16 [32, 16, 512, 512], P('dp', 'owner'), may hold values from -600 to 600
- block_layer: int32 [16], P('owner'), may hold values from 0 to 3
Outputs:
- update: bfloat16 [16, 512, 512], P('owner', 'dp')
All inputs are finite; a program needn't handle non-finite values.
Results may differ from a plain program's by a relative error of at most 0.0062.
Values may be sent and summed in bfloat16 or wider, within the bound.
A program may use at most 64 MiB of HBM per device.

v0:
```python
import jax
import jax.numpy as jnp
from jax import lax
from jax.sharding import Mesh
from jax.sharding import PartitionSpec as P

LAYERS = 4
ITERS = 3
DP = ("dp_0", "dp_1")
DP_OWNER = ("dp_0", "dp_1", "owner_0", "owner_1", "owner_2")
OWNER = ("owner_0", "owner_1", "owner_2")


def from_partner(x, axis, distance):
    return lax.ppermute(x, axis, [(i, i ^ 1 << distance) for i in range(lax.axis_size(axis))])


def cut_along(x, dim, size):
    lengths = x.shape
    parts = x.reshape(*lengths[:dim], size, lengths[dim] // size, *lengths[dim + 1 :])
    return jnp.moveaxis(parts, dim, 0)


def summed_on_arrival(x, axis, dim):
    parts = cut_along(x, dim, lax.axis_size(axis))
    arrived = lax.all_to_all(parts, axis, split_axis=0, concat_axis=0, tiled=True)
    return arrived.sum(axis=0)


def sent_to_all(x, axis):
    size = lax.axis_size(axis)
    return lax.all_to_all(jnp.broadcast_to(x[None], (size, *x.shape)), axis, 0, 0, tiled=True)


def laid_out(parts, dim):
    lengths = list(parts.shape[1:])
    lengths[dim] *= parts.shape[0]
    return jnp.moveaxis(parts, 0, dim).reshape(lengths)


def gathered_copies(x, axis, dim):
    parts = sent_to_all(x, axis)
    return laid_out(parts, dim)


def by_axis(x, axes):
    for axis in axes:
        x = lax.psum(x, axis)
    return x


def own_whole(partial_rows, position, members):
    gathered = partial_rows
    for bit_number in range(members.bit_length() - 1):
        partner = from_partner(gathered, DP, bit_number)
        upper_half = position // (1 << bit_number) % 2 == 1
        gathered = jnp.where(
            upper_half,
            jnp.concatenate([partner, gathered], axis=0),
            jnp.concatenate([gathered, partner], axis=0),
        )
    return gathered


def keep_whole(partial_rows):
    return partial_rows


def root_slab(stat_rows, eye_rows, assemble):
    size_b = stat_rows.shape[1]
    identity = jnp.eye(size_b, dtype=jnp.float32)
    statistic = assemble(stat_rows)
    ridge_term = 0.01 * jnp.trace(statistic) / size_b + 1e-06
    shifted_whole = statistic + ridge_term * identity
    scaling = jnp.sqrt(jnp.sum(shifted_whole * shifted_whole))
    current_whole = shifted_whole / scaling
    current_rows = (stat_rows + ridge_term * eye_rows) / scaling
    inverse_rows = eye_rows
    for step_number in range(ITERS):
        factor_whole = (5.0 * identity - current_whole) / 4.0
        factor_rows = (5.0 * eye_rows - current_rows) / 4.0
        if step_number == 0:
            inverse_rows = scaling ** (-0.25) * factor_rows
        else:
            inverse_rows = jnp.dot(inverse_rows, factor_whole, precision=lax.Precision.HIGHEST)
        if step_number + 1 < ITERS:
            square_rows = jnp.dot(factor_rows, factor_whole, precision=lax.Precision.HIGHEST)
            square_whole = assemble(square_rows)
            fourth_rows = jnp.dot(square_rows, square_whole, precision=lax.Precision.HIGHEST)
            current_rows = jnp.dot(fourth_rows, current_whole, precision=lax.Precision.HIGHEST)
            current_whole = assemble(current_rows)
    return inverse_rows


def per_device(gradients, block_layer):
    gradient = gradients[0, 0]
    size_b = gradient.shape[0]
    dp_count = lax.axis_size(DP)
    members = dp_count // 2
    height = size_b // members
    position = lax.axis_index(DP)
    offset = position % members * height
    left_gram = lax.dot_general(
        gradient, gradient, (((1,), (1,)), ((), ())), preferred_element_type=jnp.float32
    )
    right_gram = lax.dot_general(
        gradient, gradient, (((0,), (0,)), ((), ())), preferred_element_type=jnp.float32
    )
    stacked = jnp.concatenate([left_gram, right_gram], axis=0)
    half_rows = summed_on_arrival(stacked, DP, 0)
    statistic = own_whole(half_rows, position, members)
    inverse_whole = root_slab(statistic, jnp.eye(size_b, dtype=jnp.float32), keep_whole)
    inverse_rows = lax.dynamic_slice_in_dim(inverse_whole, offset, height, 0)
    both_roots = gathered_copies(inverse_rows.astype(jnp.bfloat16), DP, 0)
    left_root = both_roots[:size_b]
    right_root = both_roots[size_b:]
    out_height = size_b // dp_count
    right_wide = right_root.astype(jnp.float32)
    left_part = lax.slice_in_dim(left_root, 0, out_height * lax.axis_size(DP), axis=0)
    middle = jnp.dot(left_part, gradient, preferred_element_type=jnp.float32)
    summed = summed_on_arrival(jnp.dot(middle, right_wide, precision=lax.Precision.HIGHEST), DP, 0)
    precond = summed / dp_count
    layer_id = block_layer[0]
    selector = (jnp.arange(LAYERS, dtype=jnp.int32) == layer_id).astype(jnp.float32)
    energy = jnp.sum(precond * precond)
    totals_sq, counts = (
        by_axis(selector * energy, DP_OWNER),
        by_axis(selector * float(precond.size), DP_OWNER),
    )
    mean_square = jnp.sum(selector * totals_sq) / jnp.sum(selector * counts)
    update = (precond * lax.rsqrt(mean_square + 1e-06)).astype(jnp.bfloat16)
    return update[None]


def solution(mesh):
    finer = Mesh(
        mesh.devices.reshape(4, 8, 4, 2, 2), ("dp_0", "dp_1", "owner_0", "owner_1", "owner_2")
    )
    in_specs = (P(DP, OWNER, None, None), P(OWNER))
    out_specs = P(OWNER, DP, None)
    return jax.shard_map(
        per_device, mesh=finer, in_specs=in_specs, out_specs=out_specs, check_vma=False
    )
```

profile of v0, /device:TPU:1, one launch (start us, length us, event | category | flops | bytes accessed | tf_op | source)
XLA Modules:
  0.0 257.0 jit_solution(7543262102058566053)
XLA Ops:
  0.0 0.0 copy-start
  0.0 1.0 copy-done
  1.0 0.5 fusion.12
  1.5 0.5 fusion.14
  2.0 0.2 pad_maximum_fusion
  2.2 62.1 %all_to_all.15 = f32[32,32,512]{2,1,0:T(8,128)S(1)} all-to-all(f32[32,32,512]{2,1,0:T(8,128)S(1)} %bitcast.32), channel_id=1, replica_groups=mesh['dp_0'=4,'dp_1'=8,'owner_0'=4,'owner_1'=2,'owner_2'=2] {'dp_0','dp_1'}, dimensions={0} | all-to-all | bytes 4194304 | tf_op jit(solution)/shard_map/all_to_all | solution.py:26
  64.3 0.1 reduce_sum.64
  64.4 4.5 %collective-permute-start = (f32[32,512]{1,0:T(8,128)S(1)}, f32[32,512]{1,0:T(8,128)S(1)}, u32[]{:S(2)}, u32[]{:S(2)}) collective-permute-start(f32[32,512]{1,0:T(8,128)S(1)} %reduce_sum.64), channel_id=1, source_target_pairs={{0,16},{16,0},{32,48},{48,32},{64,80},{80,64},{96,112},{112,96},{1... | collective-permute-start | bytes 196616 | tf_op jit(solution)/shard_map/ppermute | solution.py:15
  68.9 1.6 collective-permute-done
  70.6 4.3 %collective-permute-start.1 = (f32[64,512]{1,0:T(8,128)S(1)}, f32[64,512]{1,0:T(8,128)S(1)}, u32[]{:S(2)}, u32[]{:S(2)}) collective-permute-start(f32[64,512]{1,0:T(8,128)S(1)} %maximum_select_fusion.3), channel_id=1, source_target_pairs={{0,32},{16,48},{32,0},{48,16},{64,96},{80,112},{96,64},{112,80},{1... | collective-permute-start | bytes 393224 | tf_op jit(solution)/shard_map/ppermute | solution.py:15
  74.9 3.7 %collective-permute-done.1 = f32[64,512]{1,0:T(8,128)S(1)} collective-permute-done((f32[64,512]{1,0:T(8,128)S(1)}, f32[64,512]{1,0:T(8,128)S(1)}, u32[]{:S(2)}, u32[]{:S(2)}) %collective-permute-start.1) | collective-permute-done | bytes 131104 | tf_op jit(solution)/shard_map/ppermute | solution.py:15
  78.7 5.4 %collective-permute-start.2 = (f32[128,512]{1,0:T(8,128)S(1)}, f32[128,512]{1,0:T(8,128)S(1)}, u32[]{:S(2)}, u32[]{:S(2)}) collective-permute-start(f32[128,512]{1,0:T(8,128)S(1)} %maximum_select_fusion.2), channel_id=1, source_target_pairs={{0,64},{16,80},{32,96},{48,112},{64,0},{80,16},{96,32},{112,48},{1... | collective-permute-start | bytes 786440 | tf_op jit(solution)/shard_map/ppermute | solution.py:15
  84.1 12.8 %collective-permute-done.2 = f32[128,512]{1,0:T(8,128)S(1)} collective-permute-done((f32[128,512]{1,0:T(8,128)S(1)}, f32[128,512]{1,0:T(8,128)S(1)}, u32[]{:S(2)}, u32[]{:S(2)}) %collective-permute-start.2) | collective-permute-done | bytes 262176 | tf_op jit(solution)/shard_map/ppermute | solution.py:15
  96.9 1.9 collective-permute-start.3
  98.9 11.8 %collective-permute-done.3 = f32[256,512]{1,0:T(8,128)S(1)} collective-permute-done((f32[256,512]{1,0:T(8,128)S(1)}, f32[256,512]{1,0:T(8,128)S(1)}, u32[]{:S(2)}, u32[]{:S(2)}) %collective-permute-start.3) | collective-permute-done | bytes 524320 | tf_op jit(solution)/shard_map/ppermute | solution.py:15
  110.7 0.0 copy-start.1
  110.7 0.7 select_reduce_fusion
  112.0 0.9 multiply_reduce_fusion
  113.6 2.1 fusion.2
  115.7 2.8 %fusion.43 = f32[512,512]{1,0:T(8,128)} fusion(f32[512,512]{1,0:T(8,128)S(1)} %fusion.2), kind=kOutput, calls=%fused_computation.56 | convolution fusion | flops 1610612736 | bytes 2097152 | tf_op jit(solution)/shard_map/dot_general | solution.py:89
  118.6 0.0 copy-done.1
  118.6 3.2 %fusion.39 = f32[512,512]{1,0:T(8,128)S(1)} fusion(f32[512,512]{1,0:T(8,128)} %fusion.43, f32[]{:T(128)S(6)} %sqrt.3, f32[]{:T(128)S(6)} %add.61, f32[256,512]{1,0:T(8,128)S(1)} %collective-permute-done.3, f32[256,512]{1,0:T(8,128)S(1)} %maximum_select_fusion.1, pred[]{:T(512)S(6)} %eq.39), kind=kOutput, calls=%fused_computation.54 | convolution fusion | flops 1612447744 | bytes 3145737 | tf_op jit(solution)/shard_map/dot_general | solution.py:90
  121.8 1.9 fusion.7
  123.7 1.8 fusion.44
  125.5 1.9 fusion
  127.4 3.3 %fusion.4 = f32[512,512]{1,0:T(8,128)S(1)} fusion(f32[512,512]{1,0:T(8,128)S(1)} %fusion.39, f32[]{:T(128)S(6)} %mul.75, f32[]{:T(128)S(6)} %sqrt.3, f32[]{:T(128)S(6)} %add.61, f32[256,512]{1,0:T(8,128)} %copy-done.1, f32[256,512]{1,0:T(8,128)S(1)} %maximum_select_fusion.1, pred[]{:T(512)S(6)} %eq.39), kind=kOutput, calls=%fused_computation.9 | convolution fusion | flops 1614282752 | bytes 3145741 | tf_op jit(solution)/shard_map/dot_general | solution.py:85
  130.7 2.0 fusion.45
  132.7 0.1 broadcast_in_dim.4
  132.9 32.6 %all_to_all.16 = bf16[32,32,512]{2,1,0:T(8,128)(2,1)S(1)} all-to-all(bf16[32,32,512]{2,1,0:T(8,128)(2,1)S(1)} %broadcast_in_dim.4), channel_id=1, replica_groups=mesh['dp_0'=4,'dp_1'=8,'owner_0'=4,'owner_1'=2,'owner_2'=2] {'dp_0','dp_1'}, dimensions={0} | all-to-all | bytes 2097152 | tf_op jit(solution)/shard_map/all_to_all | solution.py:32
  165.4 0.1 fusion.42
  165.6 0.4 fusion.10
  166.0 2.0 fusion.46
  168.0 8.0 %all-to-all-start.2 = ((f32[32,16,512]{2,1,0:T(8,128)}), f32[32,16,512]{2,1,0:T(8,128)S(1)}, u32[]{:S(2)}, u32[]{:S(2)}) async-start(f32[32,16,512]{2,1,0:T(8,128)} %fusion.46), calls=%async_computation.2 | async-start | bytes 2097152 | tf_op jit(solution)/shard_map/all_to_all | solution.py:26
  176.6 25.2 %all-to-all-done.2 = f32[32,16,512]{2,1,0:T(8,128)S(1)} async-done(((f32[32,16,512]{2,1,0:T(8,128)}), f32[32,16,512]{2,1,0:T(8,128)S(1)}, u32[]{:S(2)}, u32[]{:S(2)}) %all-to-all-start.2) | async-done | bytes 1048608 | tf_op jit(solution)/shard_map/all_to_all | solution.py:26
  201.8 0.1 reduce_sum.67
  201.8 0.6 multiply_reduce_fusion.1
  202.5 0.6 fusion.28
  203.1 10.3 %all-reduce.2 = (f32[4]{0:T(128)S(1)}, f32[4]{0:T(128)S(1)}) all-reduce(f32[4]{0:T(128)S(1)} %fusion.28, f32[4]{0:T(128)S(1)} %fusion.27), channel_id=1, replica_groups=mesh['dp_0'=4,'dp_1'=8,'owner_0'=4,'owner_1'=2,'owner_2'=2] {'dp_0'}, use_global_device_ids=true, to_apply=%region_5.6 | all-reduce | flops 8 | bytes 64 | tf_op jit(solution)/shard_map/psum | solution.py:48
  213.4 13.0 %all-reduce = (f32[4]{0:T(128)S(1)}, f32[4]{0:T(128)S(1)}) all-reduce(f32[4]{0:T(128)S(1)} %get-tuple-element.9, f32[4]{0:T(128)S(1)} %get-tuple-element.10), channel_id=1, replica_groups=mesh['dp_0'=4,'dp_1'=8,'owner_0'=4,'owner_1'=2,'owner_2'=2] {'dp_1'}, use_global_device_ids=true, to_apply=%region_6.7 | all-reduce | flops 8 | bytes 64 | tf_op jit(solution)/shard_map/psum | solution.py:48
  226.4 8.9 %all-reduce.1 = (f32[4]{0:T(128)S(1)}, f32[4]{0:T(128)S(1)}) all-reduce(f32[4]{0:T(128)S(1)} %get-tuple-element.5, f32[4]{0:T(128)S(1)} %get-tuple-element.6), channel_id=1, replica_groups=mesh['dp_0'=4,'dp_1'=8,'owner_0'=4,'owner_1'=2,'owner_2'=2] {'owner_0'}, use_global_device_ids=true, to_apply=%region_7.8 | all-reduce | flops 8 | bytes 64 | tf_op jit(solution)/shard_map/psum | solution.py:48
  235.3 7.7 %all-reduce.4 = (f32[4]{0:T(128)S(1)}, f32[4]{0:T(128)S(1)}) all-reduce(f32[4]{0:T(128)S(1)} %get-tuple-element.7, f32[4]{0:T(128)S(1)} %get-tuple-element.8), channel_id=1, replica_groups=mesh['dp_0'=4,'dp_1'=8,'owner_0'=4,'owner_1'=2,'owner_2'=2] {'owner_1'}, use_global_device_ids=true, to_apply=%region_8.9 | all-reduce | flops 8 | bytes 64 | tf_op jit(solution)/shard_map/psum | solution.py:48
  243.0 11.3 %all-reduce.3 = (f32[4]{0:T(128)S(1)}, f32[4]{0:T(128)S(1)}) all-reduce(f32[4]{0:T(128)S(1)} %get-tuple-element.13, f32[4]{0:T(128)S(1)} %get-tuple-element.14), channel_id=1, replica_groups=mesh['dp_0'=4,'dp_1'=8,'owner_0'=4,'owner_1'=2,'owner_2'=2] {'owner_2'}, use_global_device_ids=true, to_apply=%region_9.10 | all-reduce | flops 8 | bytes 64 | tf_op jit(solution)/shard_map/psum | solution.py:48
  254.3 0.7 select_reduce_fusion.1
  256.4 0.6 fusion.26
  (5 shorter events, 0.1 us)
Async XLA Ops:
  0.0 1.0 copy-start
  64.4 6.1 %collective-permute-start = (f32[32,512]{1,0:T(8,128)S(1)}, f32[32,512]{1,0:T(8,128)S(1)}, u32[]{:S(2)}, u32[]{:S(2)}) collective-permute-start(f32[32,512]{1,0:T(8,128)S(1)} %reduce_sum.64), channel_id=1, source_target_pairs={{0,16},{16,0},{32,48},{48,32},{64,80},{80,64},{96,112},{112,96},{1... | collective-permute-start | bytes 196616 | tf_op jit(solution)/shard_map/ppermute | solution.py:15
  70.6 8.1 %collective-permute-start.1 = (f32[64,512]{1,0:T(8,128)S(1)}, f32[64,512]{1,0:T(8,128)S(1)}, u32[]{:S(2)}, u32[]{:S(2)}) collective-permute-start(f32[64,512]{1,0:T(8,128)S(1)} %maximum_select_fusion.3), channel_id=1, source_target_pairs={{0,32},{16,48},{32,0},{48,16},{64,96},{80,112},{96,64},{112,80},{1... | collective-permute-start | bytes 393224 | tf_op jit(solution)/shard_map/ppermute | solution.py:15
  78.7 18.2 %collective-permute-start.2 = (f32[128,512]{1,0:T(8,128)S(1)}, f32[128,512]{1,0:T(8,128)S(1)}, u32[]{:S(2)}, u32[]{:S(2)}) collective-permute-start(f32[128,512]{1,0:T(8,128)S(1)} %maximum_select_fusion.2), channel_id=1, source_target_pairs={{0,64},{16,80},{32,96},{48,112},{64,0},{80,16},{96,32},{112,48},{1... | collective-permute-start | bytes 786440 | tf_op jit(solution)/shard_map/ppermute | solution.py:15
  96.9 13.8 %collective-permute-start.3 = (f32[256,512]{1,0:T(8,128)S(1)}, f32[256,512]{1,0:T(8,128)S(1)}, u32[]{:S(2)}, u32[]{:S(2)}) collective-permute-start(f32[256,512]{1,0:T(8,128)S(1)} %maximum_select_fusion.1), channel_id=1, source_target_pairs={{0,128},{16,144},{32,160},{48,176},{64,192},{80,208},{96,224},{112... | collective-permute-start | bytes 1572872 | tf_op jit(solution)/shard_map/ppermute | solution.py:15
  110.7 7.9 %copy-start.1 = (f32[256,512]{1,0:T(8,128)}, f32[256,512]{1,0:T(8,128)S(1)}, u32[]{:S(2)}) copy-start(f32[256,512]{1,0:T(8,128)S(1)} %collective-permute-done.3) | copy-start | bytes 1572868
  168.0 33.8 %all-to-all-start.2 = ((f32[32,16,512]{2,1,0:T(8,128)}), f32[32,16,512]{2,1,0:T(8,128)S(1)}, u32[]{:S(2)}, u32[]{:S(2)}) async-start(f32[32,16,512]{2,1,0:T(8,128)} %fusion.46), calls=%async_computation.2 | async-start | bytes 2097152 | tf_op jit(solution)/shard_map/all_to_all | solution.py:26
where the time goes:
time: 258 us; the launch traced here: 257 us
  blocking collectives  146 us (57%)
  waiting for transfers between devices  55.1 us (21%)
  starting transfers between devices  24.1 us (9%)
  matrix products  22.3 us (9%)
  other arithmetic  4.59 us (2%)
  between operations  3.79 us (1%)
    all_to_all x1, blocking collectives, summed_on_arrival(): lax.all_to_all(parts, axis, split_axis=0, concat_axis=0, tiled=True)  62.1 us
    psum x5, blocking collectives, by_axis(): x = lax.psum(x, axis)  51.1 us
    all_to_all x1, blocking collectives, sent_to_all(): lax.all_to_all(jnp.broadcast_to(x[None], (size, *x.shape)), axis, 0, 0, t...  32.6 us
    ppermute x4, waiting for transfers between devices, from_partner(): lax.ppermute(x, axis, [(i, i ^ 1 << distance) for i in range(lax.axis_siz...  29.9 us
    all_to_all x1, waiting for transfers between devices, summed_on_arrival(): lax.all_to_all(parts, axis, split_axis=0, concat_axis=0, tiled=True)  25.2 us
    ppermute x4, starting transfers between devices, from_partner(): lax.ppermute(x, axis, [(i, i ^ 1 << distance) for i in range(lax.axis_siz...  16.1 us
    all_to_all x1, starting transfers between devices, summed_on_arrival(): lax.all_to_all(parts, axis, split_axis=0, concat_axis=0, tiled=True)  7.95 us
    dot_general x2, matrix products, root_slab(): jnp.dot(inverse_rows, factor_whole, precision=lax.Precision.HIGHEST)  5.3 us
  transfers between devices with their start and end apart: 5, of which 5 were waited for; matrix products, arithmetic and copies ran while one was open for 0% of the time, Pallas kernels for 0%

commit v1 on v0

v1 whole, which is shorter than its diff:
```python
import functools

import jax
import jax.numpy as jnp
from jax import lax
from jax.experimental import pallas as pl
from jax.experimental.pallas import tpu as pltpu
from jax.sharding import Mesh
from jax.sharding import PartitionSpec as P

LAYERS = 4
MESH_ID = pl.DeviceIdType.MESH
AXES = ("y", "z", "x", "h", "c")
NY, NZ, NX, NH, NC = 4, 8, 4, 2, 2
NP = NY * NZ
NT = NP // 2
B = 512
T = 128
NB = B // T
PAIRS = tuple((i, j) for i in range(NB) for j in range(i, NB))
PACKED = len(PAIRS) * T
CHUNK = PACKED // NT
COLS = B // NT
ROWS = B // NP
F32, BF16 = jnp.float32, jnp.bfloat16
DOT = functools.partial(lax.dot_general, preferred_element_type=F32)
NN = (((1,), (0,)), ((), ()))
NTR = (((1,), (1,)), ((), ()))


def split(x):
    high = x.astype(BF16)
    return high, (x - high.astype(F32)).astype(BF16)


def product(a, b):
    return DOT(a.astype(BF16), b.astype(BF16), NN)


def spread(j, size):
    return (size + size // 2 + ((j + 1) // 2) * (1 - 2 * (j % 2))) % size


def body(
    g_ref, layer_ref, out_ref,
    packed, rs_buf, ag_send, ag_buf, gt, gt_send, s_buf, stat, n0, n1, work, corr, root,
    t_send, t_buf, p_all, p_buf, ea_send, ea_buf, eb_send, eb_buf,
    rs_s, rs_r, ag_s, ag_r, sp_s, sp_r, t_s, t_r, p_s, p_r, ea_s, ea_r, eb_s, eb_r,
):
    y, z, x = lax.axis_index("y"), lax.axis_index("z"), lax.axis_index("x")
    h, c = lax.axis_index("h"), lax.axis_index("c")
    me = y * NZ + z
    team = (y + z) % 2
    member = y * (NZ // 2) + z // 2

    def at(**place):
        where = {"y": y, "z": z, "x": x, "h": h, "c": c}
        where.update(place)
        return tuple(where[name] for name in AXES)

    def send(src, dst, send_sem, recv_sem, where):
        pltpu.make_async_remote_copy(
            src_ref=src, dst_ref=dst, send_sem=send_sem, recv_sem=recv_sem,
            device_id=where, device_id_type=MESH_ID,
        ).start()

    def wait(ref, sem):
        pltpu.make_async_copy(ref, ref, sem).wait()

    barrier = pltpu.get_barrier_semaphore()

    def greet(where):
        pl.semaphore_signal(barrier, inc=1, device_id=where, device_id_type=MESH_ID)

    @pl.loop(0, NP - 1)
    def _(k):
        greet(at(y=(y + spread(k % NY, NY)) % NY, z=(z + spread(k // NY, NZ)) % NZ))

    @pl.loop(0, NY)
    def _(k):
        greet(at(y=k, h=1 - h, c=c))
        greet(at(y=k, h=h, c=1 - c))
        greet(at(y=k, h=1 - h, c=1 - c))

    @pl.loop(0, (NX - 1) * NZ)
    def _(k):
        greet(at(x=(x + 1 + k // NZ) % NX, z=k % NZ))

    g = g_ref[0, 0]
    gt_value = g.T
    gt[...] = gt_value.astype(F32)
    for which, m in ((0, g), (1, gt_value)):
        for half in range(2):
            lo = half * (B // 2)
            panel = DOT(m[lo : lo + B // 2], m[lo:], NTR)
            for n, (i, j) in enumerate(PAIRS):
                if i // (NB // 2) == half:
                    r, q = i * T - lo, j * T - lo
                    packed[which * PACKED + n * T : which * PACKED + (n + 1) * T, :] = panel[
                        r : r + T, q : q + T
                    ].astype(BF16)

    pl.semaphore_wait(barrier, NP - 1 + 3 * NY + (NX - 1) * NZ)

    @pl.loop(0, NP - 1)
    def _(k):
        yy, zz = (y + spread(k % NY, NY)) % NY, (z + spread(k // NY, NZ)) % NZ
        first = ((yy + zz) % 2) * PACKED + (yy * (NZ // 2) + zz // 2) * CHUNK
        send(
            packed.at[pl.ds(pl.multiple_of(first, 16), CHUNK), :], rs_buf.at[me], rs_s, rs_r, at(y=yy, z=zz)
        )

    mine = pl.multiple_of(team * PACKED + member * CHUNK, 16)
    rs_buf[me] = packed[pl.ds(mine, CHUNK), :]

    @pl.loop(0, NT)
    def _(m):
        parts = [gt[pl.ds(pl.multiple_of(T * q + 8 * m, 8), 8), :] for q in range(NB)]
        gt_send[m] = jnp.concatenate(parts, axis=0).astype(BF16)

    @pl.when(team == 0)
    def _():
        s_buf[me] = gt_send[member]

    wait(rs_buf.at[pl.ds(0, NP - 1)], rs_r)
    total = rs_buf[0].astype(F32)
    for k in range(1, NP):
        total = total + rs_buf[k].astype(F32)
    ag_send[...] = total.astype(BF16)
    ag_buf[pl.ds(pl.multiple_of(member * CHUNK, 16), CHUNK), :] = total.astype(BF16)

    def teammate(k, side):
        yy = (y + spread(k % NY, NY)) % NY
        half = (z // 2 + spread(k // NY, NZ // 2)) % (NZ // 2)
        return yy, 2 * half + (side + yy) % 2

    @pl.loop(0, NT - 1)
    def _(k):
        yy, zz = teammate(k, team)
        send(
            ag_send,
            ag_buf.at[pl.ds(pl.multiple_of(member * CHUNK, 16), CHUNK), :],
            ag_s, ag_r, at(y=yy, z=zz),
        )

    @pl.loop(0, NT - 1)
    def _(k):
        yy, zz = teammate(k, 0)
        send(gt_send.at[yy * (NZ // 2) + zz // 2], s_buf.at[me], sp_s, sp_r, at(y=yy, z=zz))

    @pl.when(team == 1)
    def _():
        yy, zz = teammate(NT - 1, 0)
        send(gt_send.at[yy * (NZ // 2) + zz // 2], s_buf.at[me], sp_s, sp_r, at(y=yy, z=zz))

    wait(ag_buf.at[pl.ds(0, (NT - 1) * CHUNK), :], ag_r)

    for n, (i, j) in enumerate(PAIRS):
        block = ag_buf[n * T : (n + 1) * T, :].astype(F32)
        stat[i * T : (i + 1) * T, j * T : (j + 1) * T] = block
        if i != j:
            stat[j * T : (j + 1) * T, i * T : (i + 1) * T] = block.T
    eye = lax.broadcasted_iota(jnp.int32, (B, B), 0) == lax.broadcasted_iota(jnp.int32, (B, B), 1)
    s = stat[...]
    trace = jnp.sum(jnp.where(eye, s, 0.0), axis=(0, 1), keepdims=True)
    ridge = 0.01 * trace / B + 1e-06
    a = s + jnp.where(eye, ridge, 0.0)
    square = jnp.sum(a * a, axis=(0, 1), keepdims=True)
    scale = lax.rsqrt(square)
    n0[...] = a * (0.2 * scale)
    work[...] = product(n0[...], n0[...]) - 2.0 * n0[...]
    work[...] = product(work[...], work[...]) + 2.0 * work[...]
    n1[...] = 1.25**4 * (product(work[...], n0[...]) + n0[...])
    corr[...] = product(n0[...], n1[...]) - n0[...] - n1[...]
    work[...] = product(n1[...], n1[...]) - 2.0 * n1[...]
    work[...] = product(work[...], work[...]) + 2.0 * work[...]
    n0[...] = 1.25**4 * (product(work[...], n1[...]) + n1[...])
    factor = 1.25**3 * lax.rsqrt(jnp.sqrt(jnp.sqrt(square)))
    inverse = corr[...] - n0[...] - product(corr[...], n0[...])
    root[...] = (factor * (inverse + jnp.where(eye, 1.0, 0.0))).astype(BF16)

    @pl.when(team == 0)
    def _():
        wait(s_buf.at[pl.ds(0, NP - 1)], sp_r)
        columns = s_buf[0].astype(F32)
        for k in range(1, NP):
            columns = columns + s_buf[k].astype(F32)
        high, low = split(columns)
        turned = DOT(high, root[...], NN) + DOT(low, root[...], NN)
        lane = lax.broadcasted_iota(jnp.int32, (8, T), 1) // COLS
        for e in range(NT):
            tile = jnp.zeros((8, T), F32)
            for q in range(NB):
                part = turned[8 * q : 8 * q + 8, T * (e // NB) : T * (e // NB) + T]
                shift = (COLS * (q - e % NB)) % T
                tile = jnp.where(lane == q, pltpu.roll(part, shift, 1) if shift else part, tile)
            t_send[8 * e : 8 * e + 8, :] = tile

        @pl.loop(0, NT)
        def _(k):
            yy, zz = teammate(k, 1)
            e = yy * (NZ // 2) + zz // 2
            send(
                t_send.at[pl.ds(pl.multiple_of(8 * e, 8), 8), :],
                t_buf.at[pl.ds(pl.multiple_of(8 * member, 8), 8), :],
                t_s, t_r, at(y=yy, z=zz),
            )

        ea_send[...] = jnp.zeros((1, T), F32)
        wait(p_buf, p_r)

    @pl.when(team == 1)
    def _():
        wait(t_buf, t_r)
        turned = t_buf[...].T
        rows = jnp.concatenate([turned[COLS * q : COLS * (q + 1), :] for q in range(NB)], axis=1)
        high, low = split(rows)
        p_all[...] = (DOT(high, root[...], NN) + DOT(low, root[...], NN)) / NP
        partner = z + 1 - 2 * (z % 2)
        send(
            p_all.at[pl.ds(pl.multiple_of(ROWS * (partner % 2), ROWS), ROWS), :],
            p_buf, p_s, p_r, at(z=partner),
        )
        lane = lax.broadcasted_iota(jnp.int32, (1, T), 1)
        energy = jnp.sum(p_all[...] * p_all[...], axis=(0, 1), keepdims=True)
        here = layer_ref[0]
        ea_send[...] = jnp.where(lane == here, energy, 0.0) + jnp.where(
            lane == here + LAYERS, float(COLS * B), 0.0
        )

    place = (y * NH + h) * NC + c
    ea_buf[place] = ea_send[...]

    @pl.loop(1, NY * NH * NC)
    def _(k):
        other = (place + k) % (NY * NH * NC)
        send(
            ea_send, ea_buf.at[place], ea_s, ea_r,
            at(y=other // (NH * NC), h=other // NC % NH, c=other % NC),
        )

    wait(ea_buf.at[pl.ds(0, NY * NH * NC - 1)], ea_r)
    eb_send[...] = jnp.sum(ea_buf[...], axis=0)
    spot = x * NZ + z
    eb_buf[spot] = eb_send[...]

    @pl.loop(1, NX * NZ)
    def _(k):
        other = (spot + k) % (NX * NZ)
        send(eb_send, eb_buf.at[spot], eb_s, eb_r, at(x=other // NZ, z=other % NZ))

    @pl.when(team == 1)
    def _():
        p_buf[...] = p_all[pl.ds(pl.multiple_of(ROWS * (z % 2), ROWS), ROWS), :]

    wait(eb_buf.at[pl.ds(0, NX * NZ - 1)], eb_r)
    sums = jnp.sum(eb_buf[...], axis=0)
    lane = lax.broadcasted_iota(jnp.int32, (1, T), 1)
    here = layer_ref[0]
    layer_square = jnp.sum(jnp.where(lane == here, sums, 0.0), axis=1, keepdims=True)
    layer_count = jnp.sum(jnp.where(lane == here + LAYERS, sums, 0.0), axis=1, keepdims=True)
    out_ref[0] = (p_buf[...] * lax.rsqrt(layer_square / layer_count + 1e-06)).astype(BF16)

    wait(rs_buf.at[pl.ds(0, NP - 1)], rs_s)
    wait(ag_buf.at[pl.ds(0, (NT - 1) * CHUNK), :], ag_s)
    wait(gt_send.at[pl.ds(0, NT - 1)], sp_s)
    wait(ea_buf.at[pl.ds(0, NY * NH * NC - 1)], ea_s)
    wait(eb_buf.at[pl.ds(0, NX * NZ - 1)], eb_s)

    @pl.when(team == 0)
    def _():
        wait(t_send, t_s)

    @pl.when(team == 1)
    def _():
        wait(gt_send.at[0], sp_s)
        wait(p_buf, p_s)


def per_device(gradients, block_layer):
    return pl.pallas_call(
        body,
        out_shape=jax.ShapeDtypeStruct((1, ROWS, B), BF16),
        in_specs=[
            pl.BlockSpec(memory_space=pltpu.VMEM),
            pl.BlockSpec(memory_space=pltpu.SMEM),
        ],
        out_specs=pl.BlockSpec(memory_space=pltpu.VMEM),
        scratch_shapes=[
            pltpu.VMEM((2 * PACKED, T), BF16),
            pltpu.VMEM((NP, CHUNK, T), BF16),
            pltpu.VMEM((CHUNK, T), BF16),
            pltpu.VMEM((PACKED, T), BF16),
            pltpu.VMEM((B, B), F32),
            pltpu.VMEM((NT, COLS, B), BF16),
            pltpu.VMEM((NP, COLS, B), BF16),
            pltpu.VMEM((B, B), F32),
            pltpu.VMEM((B, B), F32),
            pltpu.VMEM((B, B), F32),
            pltpu.VMEM((B, B), F32),
            pltpu.VMEM((B, B), F32),
            pltpu.VMEM((B, B), BF16),
            pltpu.VMEM((8 * NT, T), F32),
            pltpu.VMEM((8 * NT, T), F32),
            pltpu.VMEM((COLS, B), F32),
            pltpu.VMEM((ROWS, B), F32),
            pltpu.VMEM((1, T), F32),
            pltpu.VMEM((NY * NH * NC, 1, T), F32),
            pltpu.VMEM((1, T), F32),
            pltpu.VMEM((NX * NZ, 1, T), F32),
        ]
        + [pltpu.SemaphoreType.DMA] * 14,
        compiler_params=pltpu.CompilerParams(
            collective_id=0, has_side_effects=True, vmem_limit_bytes=60 * 1024 * 1024
        ),
    )(gradients, block_layer)


def solution(mesh):
    finer = Mesh(mesh.devices.reshape(NY, NZ, NX, NH, NC), AXES)
    return jax.shard_map(
        per_device,
        mesh=finer,
        in_specs=(P(("y", "z"), ("x", "h", "c"), None, None), P(("x", "h", "c"))),
        out_specs=P(("x", "h", "c"), ("y", "z"), None),
        check_vma=False,
    )
```

time: 258 us -> 91 us (0.35)
  blocking collectives: 146 us -> 0 us
  Pallas kernels: 0 us -> 88.8 us
  waiting for transfers between devices: 55.1 us -> 0 us
  starting transfers between devices: 24.1 us -> 0 us
  matrix products: 22.3 us -> 0 us
  other arithmetic: 4.59 us -> 0 us
  between operations: 3.79 us -> 0.66 us
    all_to_all x2 -> x0, blocking collectives: 94.7 us -> none  [the longest x1 62.1 us: summed_on_arrival(): lax.all_to_all(parts, axis, split_axis=0, concat_axis=0, tiled=True)]
    pallas_call x0 -> x1, Pallas kernels: none -> 88.8 us  [per_device(): pl.pallas_call(body, out_shape=jax.ShapeDtypeStruct((1, ROWS, B), BF16),...]
    psum x5 -> x0, blocking collectives: 51.1 us -> none  [by_axis(): x = lax.psum(x, axis)]
    ppermute x4 -> x0, waiting for transfers between devices: 29.9 us -> none  [from_partner(): lax.ppermute(x, axis, [(i, i ^ 1 << distance) for i in range(lax.axis_siz...]
    all_to_all x1 -> x0, waiting for transfers between devices: 25.2 us -> none  [summed_on_arrival(): lax.all_to_all(parts, axis, split_axis=0, concat_axis=0, tiled=True)]
    dot_general x12 -> x0, matrix products: 22.3 us -> none  [the longest x2 5.3 us: root_slab(): jnp.dot(inverse_rows, factor_whole, precision=lax.Precision.HIGHEST)]
    ppermute x4 -> x0, starting transfers between devices: 16.1 us -> none  [from_partner(): lax.ppermute(x, axis, [(i, i ^ 1 << distance) for i in range(lax.axis_siz...]
    all_to_all x1 -> x0, starting transfers between devices: 7.95 us -> none  [summed_on_arrival(): lax.all_to_all(parts, axis, split_axis=0, concat_axis=0, tiled=True)]
  transfers between devices with their start and end apart: 5 -> 0, of which waited for: 5 -> 0; matrix products, arithmetic and copies ran while one was open for 0% -> 0% of each run, Pallas kernels for 0% -> 0%
where the time goes in v1:
time: 91 us; the launch traced here: 90.7 us
  Pallas kernels  88.8 us (98%)
  local copies, waits for them, and re-layouts  1.32 us (1%)
    pallas_call x1, Pallas kernels, per_device(): pl.pallas_call(body, out_shape=jax.ShapeDtypeStruct((1, ROWS, B), BF16),...  88.8 us

profile of v1, /device:TPU:1, one launch (start us, length us, event | category | flops | bytes accessed | tf_op | source)
XLA Modules:
  0.0 90.7 jit_solution(13354717922558582021)
XLA Ops:
  0.7 88.8 %shard_map.28 = bf16[1,16,512]{2,1,0:T(8,128)(2,1)} custom-call(bf16[1,1,512,512]{3,2,1,0:T(8,128)(2,1)} %g_ref.1, s32[1]{0:T(128)S(6)} %copy.4.layer_ref), custom_call_target="tpu_custom_call" | custom-call | tf_op jit(solution)/shard_map/pallas_call | solution.py:281
  89.4 1.3 %copy.5 = bf16[1,16,512]{2,1,0:T(8,128)(2,1)} copy(bf16[1,16,512]{2,1,0:T(8,128)(2,1)} %shard_map.28) | data formatting | bytes 32768

commit v2 on v1

v2 whole, which is shorter than its diff:
```python
import functools

import jax
import jax.numpy as jnp
from jax import lax
from jax.experimental import pallas as pl
from jax.experimental.pallas import tpu as pltpu
from jax.sharding import Mesh
from jax.sharding import PartitionSpec as P

LAYERS = 4
MESH_ID = pl.DeviceIdType.MESH
AXES = ("y", "z", "x", "h", "c")
NY, NZ, NX, NH, NC = 4, 8, 4, 2, 2
NP = NY * NZ
NT = NP // 2
B = 512
T = 128
NB = B // T
HALF = T // 2
PACKED = NB * (NB - 1) // 2 * T + NB * HALF + NB // 2 * HALF
CHUNK = PACKED // NT
VIA_Z = 32
VIA_Y = CHUNK - VIA_Z
COLS = B // NT
ROWS = B // NP
F32, BF16 = jnp.float32, jnp.bfloat16
DOT = functools.partial(lax.dot_general, preferred_element_type=F32)
NN = (((1,), (0,)), ((), ()))
NTR = (((1,), (1,)), ((), ()))


def split(x):
    high = x.astype(BF16)
    return high, (x - high.astype(F32)).astype(BF16)


def product(a, b):
    return DOT(a.astype(BF16), b.astype(BF16), NN)


def spread(j, size):
    return (size + size // 2 + ((j + 1) // 2) * (1 - 2 * (j % 2))) % size


def body(
    g_hbm, layer_ref, out_ref,
    g_ref, gt, packed, z_pack, y_pack, z_buf, y_buf, z_mid, y_mid, z_end, y_end,
    ag_send, ag_buf, zs_pack, ys_pack, zs_buf, ys_buf, zs_mid, ys_mid, zs_end, ys_end,
    stat, n0, n1, work, corr, root,
    t_send, t_buf, p_all, p_buf, ea_send, ea_buf, eb_send, eb_buf, sems,
):
    y, z, x = lax.axis_index("y"), lax.axis_index("z"), lax.axis_index("x")
    h, c = lax.axis_index("h"), lax.axis_index("c")
    team = (y + z) % 2
    member = y * (NZ // 2) + z // 2
    (g_sem, z1s, z1r, y1s, y1r, z2s, z2r, y2s, y2r, ags, agr, zs1s, zs1r, ys1s, ys1r,
     zs2s, zs2r, ys2s, ys2r, ts, tr, ps, pr, eas, ear, ebs, ebr) = [sems.at[k] for k in range(27)]

    def at(**place):
        where = {"y": y, "z": z, "x": x, "h": h, "c": c}
        where.update(place)
        return tuple(where[name] for name in AXES)

    def send(src, dst, send_sem, recv_sem, where):
        pltpu.make_async_remote_copy(
            src_ref=src, dst_ref=dst, send_sem=send_sem, recv_sem=recv_sem,
            device_id=where, device_id_type=MESH_ID,
        ).start()

    def wait(ref, sem):
        pltpu.make_async_copy(ref, ref, sem).wait()

    load = pltpu.make_async_copy(g_hbm.at[0, 0], g_ref, g_sem)
    load.start()

    barrier = pltpu.get_barrier_semaphore()

    def greet(where):
        pl.semaphore_signal(barrier, inc=1, device_id=where, device_id_type=MESH_ID)

    @pl.loop(0, NP - 1)
    def _(k):
        greet(at(y=(y + spread(k % NY, NY)) % NY, z=(z + spread(k // NY, NZ)) % NZ))

    @pl.loop(0, (NX - 1) * NZ)
    def _(k):
        greet(at(x=(x + 1 + k // NZ) % NX, z=(z + spread(k % NZ, NZ)) % NZ))

    @pl.loop(0, NY)
    def _(k):
        greet(at(y=k, h=1 - h, c=c))
        greet(at(y=k, h=h, c=1 - c))
        greet(at(y=k, h=1 - h, c=1 - c))

    load.wait()
    g = g_ref[...]
    gt_value = g.T
    gt[...] = gt_value.astype(F32)
    for side, m in ((0, g), (1, gt_value)):
        row = 0
        corners = []
        for half in range(2):
            lo = half * (B // 2)
            panel = DOT(m[lo : lo + B // 2], m[lo:], NTR)
            for i in range(half * NB // 2, (half + 1) * NB // 2):
                for j in range(i, NB):
                    r, q = i * T - lo, j * T - lo
                    size = HALF if i == j else T
                    packed[side, row : row + size, :] = panel[r : r + size, q : q + T]
                    row += size
                    if i == j:
                        corners.append(panel[r + HALF : r + T, q : q + T])
        lane = lax.broadcasted_iota(jnp.int32, (HALF, T), 1)
        for k in range(0, NB, 2):
            packed[side, row : row + HALF, :] = jnp.where(
                lane < HALF, pltpu.roll(corners[k], HALF, 1), corners[k + 1]
            )
            row += HALF
    for yy in range(NY):
        for zz in range(NZ):
            side, first = (yy + zz) % 2, (yy * (NZ // 2) + zz // 2) * CHUNK
            z_pack[zz, yy] = packed[side, first : first + VIA_Z, :].astype(BF16)
            y_pack[yy, zz] = packed[side, first + VIA_Z : first + CHUNK, :].astype(BF16)

    pl.semaphore_wait(barrier, NP - 1 + 3 * NY + (NX - 1) * NZ)

    def along_y(source, target, send_sem, recv_sem):
        @pl.loop(0, NY - 1)
        def _(k):
            yy = (y + spread(k, NY)) % NY
            send(source.at[yy], target.at[y], send_sem, recv_sem, at(y=yy))

    def along_z(source, target, send_sem, recv_sem):
        @pl.loop(0, NZ - 1)
        def _(k):
            zz = (z + spread(k, NZ)) % NZ
            send(source.at[zz], target.at[z], send_sem, recv_sem, at(z=zz))

    def total(ref, count):
        result = ref[0].astype(F32)
        for k in range(1, count):
            result = result + ref[k].astype(F32)
        return result

    along_y(y_pack, y_buf, y1s, y1r)
    along_z(z_pack, z_buf, z1s, z1r)
    y_buf[y] = y_pack[y]
    z_buf[z] = z_pack[z]

    def columns(m, first):
        parts = [gt[T * q + 8 * m : T * q + 8 * m + 8, :] for q in range(first, first + NB // 2)]
        return jnp.concatenate(parts, axis=0).astype(BF16)

    for zz in range(NZ):
        for k in range(NY // 2):
            zs_pack[zz, k] = columns((zz % 2 + 2 * k) * (NZ // 2) + zz // 2, 0)
    for yy in range(NY):
        for k in range(NZ // 2):
            ys_pack[yy, k] = columns(yy * (NZ // 2) + k, NB // 2)
    ys_buf[y] = ys_pack[y]
    zs_buf[z] = zs_pack[z]

    wait(z_buf.at[pl.ds(0, NZ - 1)], z1r)
    z_mid[...] = total(z_buf, NZ).astype(BF16)
    along_y(z_mid, z_end, z2s, z2r)
    z_end[y] = z_mid[y]
    wait(y_buf.at[pl.ds(0, NY - 1)], y1r)
    y_mid[...] = total(y_buf, NY).astype(BF16)
    along_z(y_mid, y_end, y2s, y2r)
    y_end[z] = y_mid[z]
    along_y(ys_pack, ys_buf, ys1s, ys1r)
    along_z(zs_pack, zs_buf, zs1s, zs1r)

    wait(z_end.at[pl.ds(0, NY - 1)], z2r)
    wait(y_end.at[pl.ds(0, NZ - 1)], y2r)
    mine = jnp.concatenate([total(z_end, NY), total(y_end, NZ)], axis=0).astype(BF16)
    ag_send[...] = mine
    ag_buf[member] = mine

    def teammate(k, side):
        yy = (y + spread(k % NY, NY)) % NY
        half = (z // 2 + spread(k // NY, NZ // 2)) % (NZ // 2)
        return yy, 2 * half + (side + yy) % 2

    @pl.loop(0, NT - 1)
    def _(k):
        yy, zz = teammate(k, team)
        send(ag_send, ag_buf.at[member], ags, agr, at(y=yy, z=zz))

    wait(zs_buf.at[pl.ds(0, NZ - 1)], zs1r)
    zs_mid[...] = total(zs_buf, NZ)
    for k in range(NY // 2):
        yy = z % 2 + 2 * k

        @pl.when(yy != y)
        def _(k=k, yy=yy):
            send(zs_mid.at[k], zs_end.at[y], zs2s, zs2r, at(y=yy))

    wait(ys_buf.at[pl.ds(0, NY - 1)], ys1r)
    ys_mid[...] = total(ys_buf, NY)
    for k in range(NZ // 2):
        zz = y % 2 + 2 * k

        @pl.when(zz != z)
        def _(k=k, zz=zz):
            send(ys_mid.at[k], ys_end.at[z], ys2s, ys2r, at(z=zz))

    wait(ag_buf.at[pl.ds(0, NT - 1)], agr)

    whole = jnp.concatenate([ag_buf[k].astype(F32) for k in range(NT)], axis=0)
    row = 0
    spare = PACKED - NB // 2 * HALF
    lower = lax.broadcasted_iota(jnp.int32, (T, T), 0) >= HALF
    left = lax.broadcasted_iota(jnp.int32, (T, T), 1) < HALF
    for i in range(NB):
        for j in range(i, NB):
            if i == j:
                corner = whole[spare + i // 2 * HALF : spare + (i // 2 + 1) * HALF]
                corner = corner if i % 2 else pltpu.roll(corner, HALF, 1)
                block = jnp.concatenate([whole[row : row + HALF], corner], axis=0)
                block = jnp.where(lower & left, block.T, block)
                row += HALF
            else:
                block = whole[row : row + T]
                stat[j * T : (j + 1) * T, i * T : (i + 1) * T] = block.T
                row += T
            stat[i * T : (i + 1) * T, j * T : (j + 1) * T] = block
    eye = lax.broadcasted_iota(jnp.int32, (B, B), 0) == lax.broadcasted_iota(jnp.int32, (B, B), 1)
    s = stat[...]
    trace = jnp.sum(jnp.where(eye, s, 0.0), axis=(0, 1), keepdims=True)
    ridge = 0.01 * trace / B + 1e-06
    a = s + jnp.where(eye, ridge, 0.0)
    square = jnp.sum(a * a, axis=(0, 1), keepdims=True)
    scale = lax.rsqrt(square)
    n0[...] = a * (0.2 * scale)
    work[...] = product(n0[...], n0[...]) - 2.0 * n0[...]
    work[...] = product(work[...], work[...]) + 2.0 * work[...]
    n1[...] = 1.25**4 * (product(work[...], n0[...]) + n0[...])
    corr[...] = product(n0[...], n1[...]) - n0[...] - n1[...]
    work[...] = product(n1[...], n1[...]) - 2.0 * n1[...]
    work[...] = product(work[...], work[...]) + 2.0 * work[...]
    n0[...] = 1.25**4 * (product(work[...], n1[...]) + n1[...])
    factor = 1.25**3 * lax.rsqrt(jnp.sqrt(jnp.sqrt(square)))
    inverse = corr[...] - n0[...] - product(corr[...], n0[...])
    root[...] = (factor * (inverse + jnp.where(eye, 1.0, 0.0))).astype(BF16)

    @pl.when(team == 0)
    def _():
        wait(zs_end.at[pl.ds(0, NY - 1)], zs2r)
        wait(ys_end.at[pl.ds(0, NZ - 1)], ys2r)
        zs_end[y] = zs_mid[y // 2]
        ys_end[z] = ys_mid[z // 2]
        summed = jnp.concatenate([total(zs_end, NY), total(ys_end, NZ)], axis=0)
        high, low = split(summed)
        turned = DOT(high, root[...], NN) + DOT(low, root[...], NN)
        lane = lax.broadcasted_iota(jnp.int32, (8, T), 1) // COLS
        for e in range(NT):
            tile = jnp.zeros((8, T), F32)
            for q in range(NB):
                part = turned[8 * q : 8 * q + 8, T * (e // NB) : T * (e // NB) + T]
                shift = (COLS * (q - e % NB)) % T
                tile = jnp.where(lane == q, pltpu.roll(part, shift, 1) if shift else part, tile)
            t_send[8 * e : 8 * e + 8, :] = tile

        @pl.loop(0, NT)
        def _(k):
            yy, zz = teammate(k, 1)
            e = yy * (NZ // 2) + zz // 2
            send(
                t_send.at[pl.ds(pl.multiple_of(8 * e, 8), 8), :],
                t_buf.at[pl.ds(pl.multiple_of(8 * member, 8), 8), :],
                ts, tr, at(y=yy, z=zz),
            )

        ea_send[...] = jnp.zeros((1, T), F32)

    @pl.when(team == 1)
    def _():
        wait(t_buf, tr)

    @pl.when(team == 1)
    def _():
        turned = t_buf[...].T
        rows = jnp.concatenate([turned[COLS * q : COLS * (q + 1), :] for q in range(NB)], axis=1)
        high, low = split(rows)
        p_all[...] = (DOT(high, root[...], NN) + DOT(low, root[...], NN)) / NP
        lane = lax.broadcasted_iota(jnp.int32, (1, T), 1)
        energy = jnp.sum(p_all[...] * p_all[...], axis=(0, 1), keepdims=True)
        here = layer_ref[0]
        ea_send[...] = jnp.where(lane == here, energy, 0.0) + jnp.where(
            lane == here + LAYERS, float(COLS * B), 0.0
        )

    place = (y * NH + h) * NC + c
    ea_buf[place] = ea_send[...]

    @pl.loop(1, NY * NH * NC)
    def _(k):
        other = (place + k) % (NY * NH * NC)
        send(
            ea_send, ea_buf.at[place], eas, ear,
            at(y=other // (NH * NC), h=other // NC % NH, c=other % NC),
        )

    @pl.when(team == 1)
    def _():
        partner = z + 1 - 2 * (z % 2)
        send(
            p_all.at[pl.ds(pl.multiple_of(ROWS * (partner % 2), ROWS), ROWS), :],
            p_buf, ps, pr, at(z=partner),
        )
        p_buf[...] = p_all[pl.ds(pl.multiple_of(ROWS * (z % 2), ROWS), ROWS), :]

    wait(ea_buf.at[pl.ds(0, NY * NH * NC - 1)], ear)
    eb_send[...] = jnp.sum(ea_buf[...], axis=0)
    spot = x * NZ + z
    eb_buf[spot] = eb_send[...]

    @pl.loop(0, NX * NZ - 1)
    def _(k):
        xx = (x + spread(k % NX, NX)) % NX
        zz = (z + spread(k // NX, NZ)) % NZ
        send(eb_send, eb_buf.at[spot], ebs, ebr, at(x=xx, z=zz))

    @pl.when(team == 0)
    def _():
        wait(p_buf, pr)

    wait(eb_buf.at[pl.ds(0, NX * NZ - 1)], ebr)
    sums = jnp.sum(eb_buf[...], axis=0)
    lane = lax.broadcasted_iota(jnp.int32, (1, T), 1)
    here = layer_ref[0]
    layer_square = jnp.sum(jnp.where(lane == here, sums, 0.0), axis=1, keepdims=True)
    layer_count = jnp.sum(jnp.where(lane == here + LAYERS, sums, 0.0), axis=1, keepdims=True)
    out_ref[0] = (p_buf[...] * lax.rsqrt(layer_square / layer_count + 1e-06)).astype(BF16)

    for ref, count, sem in (
        (y_buf, NY, y1s), (z_buf, NZ, z1s), (z_end, NY, z2s), (y_end, NZ, y2s), (ag_buf, NT, ags),
        (ys_buf, NY, ys1s), (zs_buf, NZ, zs1s), (ea_buf, NY * NH * NC, eas), (eb_buf, NX * NZ, ebs),
    ):
        wait(ref.at[pl.ds(0, count - 1)], sem)
    wait(zs_mid.at[pl.ds(0, NY // 2 - 1)], zs2s)
    wait(ys_mid.at[pl.ds(0, NZ // 2 - 1)], ys2s)

    @pl.when(team == 0)
    def _():
        wait(t_send, ts)

    @pl.when(team == 1)
    def _():
        wait(zs_mid.at[0], zs2s)
        wait(ys_mid.at[0], ys2s)
        wait(p_buf, ps)


def per_device(gradients, block_layer):
    return pl.pallas_call(
        body,
        out_shape=jax.ShapeDtypeStruct((1, ROWS, B), BF16),
        in_specs=[
            pl.BlockSpec(memory_space=pl.ANY),
            pl.BlockSpec(memory_space=pltpu.SMEM),
        ],
        out_specs=pl.BlockSpec(memory_space=pltpu.VMEM),
        scratch_shapes=[
            pltpu.VMEM((B, B), BF16),
            pltpu.VMEM((B, B), F32),
            pltpu.VMEM((2, PACKED, T), F32),
            pltpu.VMEM((NZ, NY, VIA_Z, T), BF16),
            pltpu.VMEM((NY, NZ, VIA_Y, T), BF16),
            pltpu.VMEM((NZ, NY, VIA_Z, T), BF16),
            pltpu.VMEM((NY, NZ, VIA_Y, T), BF16),
            pltpu.VMEM((NY, VIA_Z, T), BF16),
            pltpu.VMEM((NZ, VIA_Y, T), BF16),
            pltpu.VMEM((NY, VIA_Z, T), BF16),
            pltpu.VMEM((NZ, VIA_Y, T), BF16),
            pltpu.VMEM((CHUNK, T), BF16),
            pltpu.VMEM((NT, CHUNK, T), BF16),
            pltpu.VMEM((NZ, NY // 2, COLS // 2, B), BF16),
            pltpu.VMEM((NY, NZ // 2, COLS // 2, B), BF16),
            pltpu.VMEM((NZ, NY // 2, COLS // 2, B), BF16),
            pltpu.VMEM((NY, NZ // 2, COLS // 2, B), BF16),
            pltpu.VMEM((NY // 2, COLS // 2, B), F32),
            pltpu.VMEM((NZ // 2, COLS // 2, B), F32),
            pltpu.VMEM((NY, COLS // 2, B), F32),
            pltpu.VMEM((NZ, COLS // 2, B), F32),
        ]
        + [pltpu.VMEM((B, B), F32)] * 5
        + [
            pltpu.VMEM((B, B), BF16),
            pltpu.VMEM((8 * NT, T), F32),
            pltpu.VMEM((8 * NT, T), F32),
            pltpu.VMEM((COLS, B), F32),
            pltpu.VMEM((ROWS, B), F32),
            pltpu.VMEM((1, T), F32),
            pltpu.VMEM((NY * NH * NC, 1, T), F32),
            pltpu.VMEM((1, T), F32),
            pltpu.VMEM((NX * NZ, 1, T), F32),
            pltpu.SemaphoreType.DMA((27,)),
        ],
        compiler_params=pltpu.CompilerParams(
            collective_id=0, has_side_effects=True, vmem_limit_bytes=60 * 1024 * 1024
        ),
    )(gradients, block_layer)


def solution(mesh):
    finer = Mesh(mesh.devices.reshape(NY, NZ, NX, NH, NC), AXES)
    return jax.shard_map(
        per_device,
        mesh=finer,
        in_specs=(P(("y", "z"), ("x", "h", "c"), None, None), P(("x", "h", "c"))),
        out_specs=P(("x", "h", "c"), ("y", "z"), None),
        check_vma=False,
    )
```

time: 91 us -> 66.9 us (0.74)
  Pallas kernels: 88.8 us -> 64.7 us
    pallas_call x1, Pallas kernels: 88.8 us -> 64.7 us  [per_device(): pl.pallas_call(body, out_shape=jax.ShapeDtypeStruct((1, ROWS, B), BF16),...]
where the time goes in v2:
time: 66.9 us; the launch traced here: 66.7 us
  Pallas kernels  64.7 us (97%)
  local copies, waits for them, and re-layouts  1.32 us (2%)
    pallas_call x1, Pallas kernels, per_device(): pl.pallas_call(body, out_shape=jax.ShapeDtypeStruct((1, ROWS, B), BF16),...  64.7 us

profile of v2, /device:TPU:1, one launch (start us, length us, event | category | flops | bytes accessed | tf_op | source)
XLA Modules:
  0.0 66.7 jit_solution(17797072217524694115)
XLA Ops:
  0.7 64.7 %shard_map.28 = bf16[1,16,512]{2,1,0:T(8,128)(2,1)} custom-call(bf16[1,1,512,512]{3,2,1,0:T(8,128)(2,1)} %g_hbm.1, s32[1]{0:T(128)S(6)} %copy.4.layer_ref), custom_call_target="tpu_custom_call" | custom-call | tf_op jit(solution)/shard_map/pallas_call | solution.py:358
  65.4 1.3 %copy.5 = bf16[1,16,512]{2,1,0:T(8,128)(2,1)} copy(bf16[1,16,512]{2,1,0:T(8,128)(2,1)} %shard_map.28) | data formatting | bytes 32768

commit v3 on v2

--- a/solution.py
+++ b/solution.py
@@ -39,23 +39,33 @@
     return DOT(a.astype(BF16), b.astype(BF16), NN)
 
 
-def spread(j, size):
-    return (size + size // 2 + ((j + 1) // 2) * (1 - 2 * (j % 2))) % size
+def spread(size):
+    return sorted(range(size), key=lambda d: -min(d, size - d))
+
+
+def pairs_of(first, second):
+    far = [(a, b) for a in spread(first) for b in spread(second)]
+    return sorted(far, key=lambda p: -min(p[0], first - p[0]) - min(p[1], second - p[1]))
 
 
 def body(
-    g_hbm, layer_ref, out_ref,
+    g_hbm, layer_hbm, out_ref,
     g_ref, gt, packed, z_pack, y_pack, z_buf, y_buf, z_mid, y_mid, z_end, y_end,
     ag_send, ag_buf, zs_pack, ys_pack, zs_buf, ys_buf, zs_mid, ys_mid, zs_end, ys_end,
     stat, n0, n1, work, corr, root,
-    t_send, t_buf, p_all, p_buf, ea_send, ea_buf, eb_send, eb_buf, sems,
+    t_send, t_buf, p_all, p_buf, ea_send, ea_buf, eb_send, eb_buf, layer_ref, sems,
 ):
     y, z, x = lax.axis_index("y"), lax.axis_index("z"), lax.axis_index("x")
     h, c = lax.axis_index("h"), lax.axis_index("c")
     team = (y + z) % 2
-    member = y * (NZ // 2) + z // 2
+    member = y * (NZ // 2) + lax.div(z, 2)
+    ys = [lax.rem(y + d, NY) for d in range(NY)]
+    zs = [lax.rem(z + d, NZ) for d in range(NZ)]
+    xs = [lax.rem(x + d, NX) for d in range(NX)]
+    halves = [lax.rem(lax.div(z, 2) + d, NZ // 2) for d in range(NZ // 2)]
     (g_sem, z1s, z1r, y1s, y1r, z2s, z2r, y2s, y2r, ags, agr, zs1s, zs1r, ys1s, ys1r,
      zs2s, zs2r, ys2s, ys2r, ts, tr, ps, pr, eas, ear, ebs, ebr) = [sems.at[k] for k in range(27)]
+    layer_sem = sems.at[27]
 
     def at(**place):
         where = {"y": y, "z": z, "x": x, "h": h, "c": c}
@@ -73,27 +83,26 @@
 
     load = pltpu.make_async_copy(g_hbm.at[0, 0], g_ref, g_sem)
     load.start()
+    load_layer = pltpu.make_async_copy(layer_hbm, layer_ref, layer_sem)
+    load_layer.start()
 
     barrier = pltpu.get_barrier_semaphore()
 
     def greet(where):
         pl.semaphore_signal(barrier, inc=1, device_id=where, device_id_type=MESH_ID)
 
-    @pl.loop(0, NP - 1)
-    def _(k):
-        greet(at(y=(y + spread(k % NY, NY)) % NY, z=(z + spread(k // NY, NZ)) % NZ))
-
-    @pl.loop(0, (NX - 1) * NZ)
-    def _(k):
-        greet(at(x=(x + 1 + k // NZ) % NX, z=(z + spread(k % NZ, NZ)) % NZ))
-
-    @pl.loop(0, NY)
-    def _(k):
-        greet(at(y=k, h=1 - h, c=c))
-        greet(at(y=k, h=h, c=1 - c))
-        greet(at(y=k, h=1 - h, c=1 - c))
+    for dx, dz in pairs_of(NX, NZ):
+        if dx:
+            greet(at(x=xs[dx], z=zs[dz]))
+    for dy in spread(NY):
+        greet(at(y=ys[dy], h=1 - h, c=c))
+        greet(at(y=ys[dy], h=h, c=1 - c))
+        greet(at(y=ys[dy], h=1 - h, c=1 - c))
+    for dy, dz in pairs_of(NY, NZ)[:-1]:
+        greet(at(y=ys[dy], z=zs[dz]))
 
     load.wait()
+    load_layer.wait()
     g = g_ref[...]
     gt_value = g.T
     gt[...] = gt_value.astype(F32)
@@ -126,16 +135,12 @@
     pl.semaphore_wait(barrier, NP - 1 + 3 * NY + (NX - 1) * NZ)
 
     def along_y(source, target, send_sem, recv_sem):
-        @pl.loop(0, NY - 1)
-        def _(k):
-            yy = (y + spread(k, NY)) % NY
-            send(source.at[yy], target.at[y], send_sem, recv_sem, at(y=yy))
+        for d in spread(NY)[:-1]:
+            send(source.at[ys[d]], target.at[y], send_sem, recv_sem, at(y=ys[d]))
 
     def along_z(source, target, send_sem, recv_sem):
-        @pl.loop(0, NZ - 1)
-        def _(k):
-            zz = (z + spread(k, NZ)) % NZ
-            send(source.at[zz], target.at[z], send_sem, recv_sem, at(z=zz))
+        for d in spread(NZ)[:-1]:
+            send(source.at[zs[d]], target.at[z], send_sem, recv_sem, at(z=zs[d]))
 
     def total(ref, count):
         result = ref[0].astype(F32)
@@ -161,6 +166,9 @@
     ys_buf[y] = ys_pack[y]
     zs_buf[z] = zs_pack[z]
 
+    along_y(ys_pack, ys_buf, ys1s, ys1r)
+    along_z(zs_pack, zs_buf, zs1s, zs1r)
+
     wait(z_buf.at[pl.ds(0, NZ - 1)], z1r)
     z_mid[...] = total(z_buf, NZ).astype(BF16)
     along_y(z_mid, z_end, z2s, z2r)
@@ -169,24 +177,15 @@
     y_mid[...] = total(y_buf, NY).astype(BF16)
     along_z(y_mid, y_end, y2s, y2r)
     y_end[z] = y_mid[z]
-    along_y(ys_pack, ys_buf, ys1s, ys1r)
-    along_z(zs_pack, zs_buf, zs1s, zs1r)
-
     wait(z_end.at[pl.ds(0, NY - 1)], z2r)
     wait(y_end.at[pl.ds(0, NZ - 1)], y2r)
     mine = jnp.concatenate([total(z_end, NY), total(y_end, NZ)], axis=0).astype(BF16)
     ag_send[...] = mine
     ag_buf[member] = mine
 
-    def teammate(k, side):
-        yy = (y + spread(k % NY, NY)) % NY
-        half = (z // 2 + spread(k // NY, NZ // 2)) % (NZ // 2)
-        return yy, 2 * half + (side + yy) % 2
-
-    @pl.loop(0, NT - 1)
-    def _(k):
-        yy, zz = teammate(k, team)
-        send(ag_send, ag_buf.at[member], ags, agr, at(y=yy, z=zz))
+    for dy, dh in pairs_of(NY, NZ // 2)[:-1]:
+        zz = 2 * halves[dh] + lax.rem(team + ys[dy], 2)
+        send(ag_send, ag_buf.at[member], ags, agr, at(y=ys[dy], z=zz))
 
     wait(zs_buf.at[pl.ds(0, NZ - 1)], zs1r)
     zs_mid[...] = total(zs_buf, NZ)
@@ -263,14 +262,12 @@
                 tile = jnp.where(lane == q, pltpu.roll(part, shift, 1) if shift else part, tile)
             t_send[8 * e : 8 * e + 8, :] = tile
 
-        @pl.loop(0, NT)
-        def _(k):
-            yy, zz = teammate(k, 1)
-            e = yy * (NZ // 2) + zz // 2
+        for dy, dh in pairs_of(NY, NZ // 2):
+            e = ys[dy] * (NZ // 2) + halves[dh]
             send(
                 t_send.at[pl.ds(pl.multiple_of(8 * e, 8), 8), :],
                 t_buf.at[pl.ds(pl.multiple_of(8 * member, 8), 8), :],
-                ts, tr, at(y=yy, z=zz),
+                ts, tr, at(y=ys[dy], z=2 * halves[dh] + lax.rem(1 + ys[dy], 2)),
             )
 
         ea_send[...] = jnp.zeros((1, T), F32)
@@ -295,13 +292,11 @@
     place = (y * NH + h) * NC + c
     ea_buf[place] = ea_send[...]
 
-    @pl.loop(1, NY * NH * NC)
-    def _(k):
-        other = (place + k) % (NY * NH * NC)
-        send(
-            ea_send, ea_buf.at[place], eas, ear,
-            at(y=other // (NH * NC), h=other // NC % NH, c=other % NC),
-        )
+    for hh in (1 - h, h):
+        for dy in spread(NY):
+            for cc in (1 - c, c):
+                if not (hh is h and cc is c and dy == 0):
+                    send(ea_send, ea_buf.at[place], eas, ear, at(y=ys[dy], h=hh, c=cc))
 
     @pl.when(team == 1)
     def _():
@@ -317,11 +312,8 @@
     spot = x * NZ + z
     eb_buf[spot] = eb_send[...]
 
-    @pl.loop(0, NX * NZ - 1)
-    def _(k):
-        xx = (x + spread(k % NX, NX)) % NX
-        zz = (z + spread(k // NX, NZ)) % NZ
-        send(eb_send, eb_buf.at[spot], ebs, ebr, at(x=xx, z=zz))
+    for dx, dz in pairs_of(NX, NZ)[:-1]:
+        send(eb_send, eb_buf.at[spot], ebs, ebr, at(x=xs[dx], z=zs[dz]))
 
     @pl.when(team == 0)
     def _():
@@ -360,7 +352,7 @@
         out_shape=jax.ShapeDtypeStruct((1, ROWS, B), BF16),
         in_specs=[
             pl.BlockSpec(memory_space=pl.ANY),
-            pl.BlockSpec(memory_space=pltpu.SMEM),
+            pl.BlockSpec(memory_space=pl.ANY),
         ],
         out_specs=pl.BlockSpec(memory_space=pltpu.VMEM),
         scratch_shapes=[
@@ -397,7 +389,8 @@
             pltpu.VMEM((NY * NH * NC, 1, T), F32),
             pltpu.VMEM((1, T), F32),
             pltpu.VMEM((NX * NZ, 1, T), F32),
-            pltpu.SemaphoreType.DMA((27,)),
+            pltpu.SMEM((1,), jnp.int32),
+            pltpu.SemaphoreType.DMA((28,)),
         ],
         compiler_params=pltpu.CompilerParams(
             collective_id=0, has_side_effects=True, vmem_limit_bytes=60 * 1024 * 1024

time: 66.9 us -> 64.4 us (0.963)
  Pallas kernels: 64.7 us -> 62.2 us
    pallas_call x1, Pallas kernels: 64.7 us -> 62.2 us  [per_device(): pl.pallas_call(body, out_shape=jax.ShapeDtypeStruct((1, ROWS, B), BF16),...]
where the time goes in v3:
time: 64.4 us; the launch traced here: 64.2 us
  Pallas kernels  62.2 us (97%)
  local copies, waits for them, and re-layouts  1.32 us (2%)
  between operations  0.66 us (1%)
    pallas_call x1, Pallas kernels, per_device(): pl.pallas_call(body, out_shape=jax.ShapeDtypeStruct((1, ROWS, B), BF16),...  62.2 us
    unnamed x1, local copies, waits for them, and re-layouts  1.32 us

profile of v3, /device:TPU:1, one launch (start us, length us, event | category | flops | bytes accessed | tf_op | source)
XLA Modules:
  0.0 64.2 jit_solution(3579446731809766793)
XLA Ops:
  0.7 62.2 %shard_map.28 = bf16[1,16,512]{2,1,0:T(8,128)(2,1)} custom-call(bf16[1,1,512,512]{3,2,1,0:T(8,128)(2,1)} %g_hbm.1, s32[1]{0:T(128)S(6)} %copy.4.layer_hbm), custom_call_target="tpu_custom_call" | custom-call | tf_op jit(solution)/shard_map/pallas_call | solution.py:350
  62.9 1.3 %copy.5 = bf16[1,16,512]{2,1,0:T(8,128)(2,1)} copy(bf16[1,16,512]{2,1,0:T(8,128)(2,1)} %shard_map.28) | data formatting | bytes 32768

commit v4 on v3

--- a/solution.py
+++ b/solution.py
@@ -91,6 +91,8 @@
     def greet(where):
         pl.semaphore_signal(barrier, inc=1, device_id=where, device_id_type=MESH_ID)
 
+    for dy, dz in pairs_of(NY, NZ)[:-1]:
+        greet(at(y=ys[dy], z=zs[dz]))
     for dx, dz in pairs_of(NX, NZ):
         if dx:
             greet(at(x=xs[dx], z=zs[dz]))
@@ -98,8 +100,6 @@
         greet(at(y=ys[dy], h=1 - h, c=c))
         greet(at(y=ys[dy], h=h, c=1 - c))
         greet(at(y=ys[dy], h=1 - h, c=1 - c))
-    for dy, dz in pairs_of(NY, NZ)[:-1]:
-        greet(at(y=ys[dy], z=zs[dz]))
 
     load.wait()
     load_layer.wait()
@@ -169,14 +169,14 @@
     along_y(ys_pack, ys_buf, ys1s, ys1r)
     along_z(zs_pack, zs_buf, zs1s, zs1r)
 
+    wait(y_buf.at[pl.ds(0, NY - 1)], y1r)
+    y_mid[...] = total(y_buf, NY).astype(BF16)
+    along_z(y_mid, y_end, y2s, y2r)
+    y_end[z] = y_mid[z]
     wait(z_buf.at[pl.ds(0, NZ - 1)], z1r)
     z_mid[...] = total(z_buf, NZ).astype(BF16)
     along_y(z_mid, z_end, z2s, z2r)
     z_end[y] = z_mid[y]
-    wait(y_buf.at[pl.ds(0, NY - 1)], y1r)
-    y_mid[...] = total(y_buf, NY).astype(BF16)
-    along_z(y_mid, y_end, y2s, y2r)
-    y_end[z] = y_mid[z]
     wait(z_end.at[pl.ds(0, NY - 1)], z2r)
     wait(y_end.at[pl.ds(0, NZ - 1)], y2r)
     mine = jnp.concatenate([total(z_end, NY), total(y_end, NZ)], axis=0).astype(BF16)
@@ -349,10 +349,10 @@
 def per_device(gradients, block_layer):
     return pl.pallas_call(
         body,
-        out_shape=jax.ShapeDtypeStruct((1, ROWS, B), BF16),
+        out_shape=pltpu.VMEM((1, ROWS, B), BF16),
         in_specs=[
-            pl.BlockSpec(memory_space=pl.ANY),
-            pl.BlockSpec(memory_space=pl.ANY),
+            pl.BlockSpec(memory_space=pltpu.HBM),
+            pl.BlockSpec(memory_space=pltpu.HBM),
         ],
         out_specs=pl.BlockSpec(memory_space=pltpu.VMEM),
         scratch_shapes=[

time: 64.4 us -> 62.6 us (0.972)
  Pallas kernels: 62.2 us -> 61.2 us
  local copies, waits for them, and re-layouts: 1.32 us -> 0.61 us
    pallas_call x1, Pallas kernels: 62.2 us -> 61.2 us  [per_device(): pl.pallas_call(body, out_shape=pltpu.VMEM((1, ROWS, B), BF16), in_specs=[...]
    unnamed x1, local copies, waits for them, and re-layouts: 1.32 us -> 0.61 us
where the time goes in v4:
time: 62.6 us; the launch traced here: 62.5 us
  Pallas kernels  61.2 us (98%)
  between operations  0.66 us (1%)
    pallas_call x1, Pallas kernels, per_device(): pl.pallas_call(body, out_shape=pltpu.VMEM((1, ROWS, B), BF16), in_specs=[...  61.2 us

profile of v4, /device:TPU:1, one launch (start us, length us, event | category | flops | bytes accessed | tf_op | source)
XLA Modules:
  0.0 62.5 jit_solution(9563890178716178507)
XLA Ops:
  0.7 61.2 %shard_map.28 = bf16[1,16,512]{2,1,0:T(8,128)(2,1)S(1)} custom-call(bf16[1,1,512,512]{3,2,1,0:T(8,128)(2,1)} %g_hbm.1, s32[1]{0:T(128)S(6)} %copy.5.layer_hbm), custom_call_target="tpu_custom_call" | custom-call | tf_op jit(solution)/shard_map/pallas_call | solution.py:350
  61.9 0.6 copy.4

commit v5 on v4

--- a/solution.py
+++ b/solution.py
@@ -30,9 +30,9 @@
 NTR = (((1,), (1,)), ((), ()))
 
 
-def split(x):
+def stacked(x):
     high = x.astype(BF16)
-    return high, (x - high.astype(F32)).astype(BF16)
+    return jnp.concatenate([high, (x - high.astype(F32)).astype(BF16)], axis=0)
 
 
 def product(a, b):
@@ -52,7 +52,7 @@
     g_hbm, layer_hbm, out_ref,
     g_ref, gt, packed, z_pack, y_pack, z_buf, y_buf, z_mid, y_mid, z_end, y_end,
     ag_send, ag_buf, zs_pack, ys_pack, zs_buf, ys_buf, zs_mid, ys_mid, zs_end, ys_end,
-    stat, n0, n1, work, corr, root,
+    n0, n1, work, corr, root,
     t_send, t_buf, p_all, p_buf, ea_send, ea_buf, eb_send, eb_buf, layer_ref, sems,
 ):
     y, z, x = lax.axis_index("y"), lax.axis_index("z"), lax.axis_index("x")
@@ -91,8 +91,6 @@
     def greet(where):
         pl.semaphore_signal(barrier, inc=1, device_id=where, device_id_type=MESH_ID)
 
-    for dy, dz in pairs_of(NY, NZ)[:-1]:
-        greet(at(y=ys[dy], z=zs[dz]))
     for dx, dz in pairs_of(NX, NZ):
         if dx:
             greet(at(x=xs[dx], z=zs[dz]))
@@ -100,6 +98,8 @@
         greet(at(y=ys[dy], h=1 - h, c=c))
         greet(at(y=ys[dy], h=h, c=1 - c))
         greet(at(y=ys[dy], h=1 - h, c=1 - c))
+    for dy, dz in pairs_of(NY, NZ)[:-1]:
+        greet(at(y=ys[dy], z=zs[dz]))
 
     load.wait()
     load_layer.wait()
@@ -208,31 +208,47 @@
     wait(ag_buf.at[pl.ds(0, NT - 1)], agr)
 
     whole = jnp.concatenate([ag_buf[k].astype(F32) for k in range(NT)], axis=0)
+    spare = PACKED - NB // 2 * HALF
+    diagonal, off_diagonal, corners = [], {}, []
     row = 0
-    spare = PACKED - NB // 2 * HALF
-    lower = lax.broadcasted_iota(jnp.int32, (T, T), 0) >= HALF
-    left = lax.broadcasted_iota(jnp.int32, (T, T), 1) < HALF
     for i in range(NB):
         for j in range(i, NB):
             if i == j:
-                corner = whole[spare + i // 2 * HALF : spare + (i // 2 + 1) * HALF]
-                corner = corner if i % 2 else pltpu.roll(corner, HALF, 1)
-                block = jnp.concatenate([whole[row : row + HALF], corner], axis=0)
-                block = jnp.where(lower & left, block.T, block)
+                diagonal.append(whole[row : row + HALF])
                 row += HALF
             else:
-                block = whole[row : row + T]
-                stat[j * T : (j + 1) * T, i * T : (i + 1) * T] = block.T
+                off_diagonal[i, j] = whole[row : row + T]
                 row += T
-            stat[i * T : (i + 1) * T, j * T : (j + 1) * T] = block
+    for i in range(NB // 2):
+        corners.append(whole[spare + i * HALF : spare + (i + 1) * HALF])
+    down = lax.broadcasted_iota(jnp.int32, (HALF, T), 0)
+    across = lax.broadcasted_iota(jnp.int32, (HALF, T), 1)
+
+    def added(x):
+        return jnp.sum(x.reshape(-1, 8, T), axis=0)
+
+    squares = sum(2.0 * added(block * block) for block in off_diagonal.values())
+    squares += sum(added(jnp.where(across < HALF, 1.0, 2.0) * block * block) for block in diagonal)
+    squares += sum(added(block * block) for block in corners)
+    traces = sum(added(jnp.where(across == down, block, 0.0)) for block in diagonal)
+    traces += sum(added(jnp.where(across % HALF == down, block, 0.0)) for block in corners)
+    trace = jnp.sum(traces, axis=(0, 1), keepdims=True)
+    ridge = 0.01 * trace / B + 1e-06
+    square = jnp.sum(squares, axis=(0, 1), keepdims=True) + ridge * (2.0 * trace + B * ridge)
+    scale = 0.2 * lax.rsqrt(square)
+    lower = lax.broadcasted_iota(jnp.int32, (T, T), 0) >= HALF
+    left = lax.broadcasted_iota(jnp.int32, (T, T), 1) < HALF
+    unit = lax.broadcasted_iota(jnp.int32, (T, T), 0) == lax.broadcasted_iota(jnp.int32, (T, T), 1)
+    for (i, j), block in off_diagonal.items():
+        block = block * scale
+        n0[i * T : (i + 1) * T, j * T : (j + 1) * T] = block
+        n0[j * T : (j + 1) * T, i * T : (i + 1) * T] = block.T
+    for i in range(NB):
+        corner = corners[i // 2] if i % 2 else pltpu.roll(corners[i // 2], HALF, 1)
+        block = jnp.concatenate([diagonal[i], corner], axis=0)
+        block = jnp.where(lower & left, block.T, block)
+        n0[i * T : (i + 1) * T, i * T : (i + 1) * T] = (block + jnp.where(unit, ridge, 0.0)) * scale
     eye = lax.broadcasted_iota(jnp.int32, (B, B), 0) == lax.broadcasted_iota(jnp.int32, (B, B), 1)
-    s = stat[...]
-    trace = jnp.sum(jnp.where(eye, s, 0.0), axis=(0, 1), keepdims=True)
-    ridge = 0.01 * trace / B + 1e-06
-    a = s + jnp.where(eye, ridge, 0.0)
-    square = jnp.sum(a * a, axis=(0, 1), keepdims=True)
-    scale = lax.rsqrt(square)
-    n0[...] = a * (0.2 * scale)
     work[...] = product(n0[...], n0[...]) - 2.0 * n0[...]
     work[...] = product(work[...], work[...]) + 2.0 * work[...]
     n1[...] = 1.25**4 * (product(work[...], n0[...]) + n0[...])
@@ -251,8 +267,8 @@
         zs_end[y] = zs_mid[y // 2]
         ys_end[z] = ys_mid[z // 2]
         summed = jnp.concatenate([total(zs_end, NY), total(ys_end, NZ)], axis=0)
-        high, low = split(summed)
-        turned = DOT(high, root[...], NN) + DOT(low, root[...], NN)
+        both = DOT(stacked(summed), root[...], NN)
+        turned = both[:COLS] + both[COLS:]
         lane = lax.broadcasted_iota(jnp.int32, (8, T), 1) // COLS
         for e in range(NT):
             tile = jnp.zeros((8, T), F32)
@@ -280,8 +296,8 @@
     def _():
         turned = t_buf[...].T
         rows = jnp.concatenate([turned[COLS * q : COLS * (q + 1), :] for q in range(NB)], axis=1)
-        high, low = split(rows)
-        p_all[...] = (DOT(high, root[...], NN) + DOT(low, root[...], NN)) / NP
+        both = DOT(stacked(rows), root[...], NN)
+        p_all[...] = (both[:COLS] + both[COLS:]) * (1.0 / NP)
         lane = lax.broadcasted_iota(jnp.int32, (1, T), 1)
         energy = jnp.sum(p_all[...] * p_all[...], axis=(0, 1), keepdims=True)
         here = layer_ref[0]
@@ -378,7 +394,7 @@
             pltpu.VMEM((NY, COLS // 2, B), F32),
             pltpu.VMEM((NZ, COLS // 2, B), F32),
         ]
-        + [pltpu.VMEM((B, B), F32)] * 5
+        + [pltpu.VMEM((B, B), F32)] * 4
         + [
             pltpu.VMEM((B, B), BF16),
             pltpu.VMEM((8 * NT, T), F32),

time: 62.6 us -> 62.5 us (level)
  no operation moved by 1% of the time
where the time goes in v5:
time: 62.5 us; the launch traced here: 62.3 us
  Pallas kernels  61.1 us (98%)
  between operations  0.66 us (1%)
    pallas_call x1, Pallas kernels, per_device(): pl.pallas_call(body, out_shape=pltpu.VMEM((1, ROWS, B), BF16), in_specs=[...  61.1 us

profile of v5, /device:TPU:1, one launch (start us, length us, event | category | flops | bytes accessed | tf_op | source)
XLA Modules:
  0.0 62.3 jit_solution(9061996844882473922)
XLA Ops:
  0.7 61.1 %shard_map.28 = bf16[1,16,512]{2,1,0:T(8,128)(2,1)S(1)} custom-call(bf16[1,1,512,512]{3,2,1,0:T(8,128)(2,1)} %g_hbm.1, s32[1]{0:T(128)S(6)} %copy.5.layer_hbm), custom_call_target="tpu_custom_call" | custom-call | tf_op jit(solution)/shard_map/pallas_call | solution.py:366
  61.7 0.6 copy.4
